TPU v7x, 128 devices: a whole 4x4x4 slice. The times are simulated.
128 devices in a mesh: dp: 8 (over y_lo, x), tensor: 16 (over z, y_hi, core).
Axes of the slice: x: 4, y: 4 (y_hi: 2, y_lo: 2; y = y_hi * 2 + y_lo), z: 4, core: 2. Of those that a mesh axis runs over, the one named last changes fastest.
Arguments:
- tokens: bfloat16 [8192, 2048], P(('dp', 'tensor')), may hold values from -12 to 12
- targets: bfloat16 [8192, 2048], P(('dp', 'tensor')), may hold values from -6 to 6
- learner_gain: float32 [2048], replicated, may hold values from 0.1 to 1.9
- learner_gate: bfloat16 [2048, 8192], P(None, 'tensor'), may hold values from -0.125 to 0.125
- learner_up: bfloat16 [2048, 8192], P(None, 'tensor'), may hold values from -0.125 to 0.125
- learner_down: bfloat16 [8192, 2048], P('tensor'), may hold values from -0.0625 to 0.0625
- frozen_gain: float32 [2048], replicated, may hold values from 0.1 to 1.9
- frozen_gate: bfloat16 [2048, 8192], P(None, 'tensor'), may hold values from -0.125 to 0.125
- frozen_up: bfloat16 [2048, 8192], P(None, 'tensor'), may hold values from -0.125 to 0.125
- frozen_down: bfloat16 [8192, 2048], P('tensor'), may hold values from -0.0625 to 0.0625
Outputs:
- scores: float32 [8192], P(('dp', 'tensor'))
- grad_tokens: bfloat16 [8192, 2048], P(('dp', 'tensor'))
- grad_gain: float32 [2048], replicated
- grad_gate: float32 [2048, 8192], P('dp', 'tensor')
- grad_up: float32 [2048, 8192], P('dp', 'tensor')
- grad_down: float32 [8192, 2048], P('tensor', 'dp')
All inputs are finite; a program needn't handle non-finite values.
Results may differ from a plain program's by a relative error of at most 0.0096.
Values may be sent and summed in bfloat16 or wider, within the bound.
A program may use at most 128 MiB of HBM per device.

v0:
```python
import math
import jax
import jax.numpy as jnp
from jax import lax
from jax.sharding import PartitionSpec as P


def in_one_piece(arrays, axis, dim, along):
    both = jnp.concatenate(arrays, axis=along)
    out, at, gathered = (lax.all_gather(both, axis, axis=dim, tiled=True), 0, [])
    for a in arrays:
        gathered.append(lax.slice_in_dim(out, at, at + a.shape[along], axis=along))
        at += a.shape[along]
    return tuple(gathered)


def split_up(value, dim, size):
    shape = value.shape
    blocks = value.reshape(*shape[:dim], size, shape[dim] // size, *shape[dim + 1 :])
    return jnp.moveaxis(blocks, dim, 0)


def sum_at_owner(value, axis, dim):
    blocks = split_up(value, dim, lax.axis_size(axis))
    arrived = lax.all_to_all(blocks, axis, split_axis=0, concat_axis=0, tiled=True)
    return arrived.astype(jnp.float32).sum(axis=0)


def sent_together(arrays, axis, dim, along):
    widths = [a.shape[along] for a in arrays]
    both = jnp.concatenate(arrays, axis=along)
    out = sum_at_owner(both, axis, dim)
    return tuple(jnp.split(out, [sum(widths[:k]) for k in range(1, len(widths))], axis=along))


def project_up(normed, w_gate, w_up, w_down):
    gate_pre = jnp.dot(normed, w_gate, preferred_element_type=jnp.float32)
    up_pre = jnp.dot(normed, w_up, preferred_element_type=jnp.float32)
    hidden = (jax.nn.silu(gate_pre) * up_pre).astype(jnp.bfloat16)
    partial_out = jnp.dot(hidden, w_down, preferred_element_type=jnp.float32)
    return (gate_pre, up_pre, hidden, partial_out)


def local(
    tokens,
    targets,
    learner_gain,
    learner_gate,
    learner_up,
    learner_down,
    frozen_gain,
    frozen_gate,
    frozen_up,
    frozen_down,
):
    xfloat = tokens.astype(jnp.float32)
    inv_rms = lax.rsqrt(jnp.mean(xfloat * xfloat, axis=-1, keepdims=True) + 1e-05)
    normed = (xfloat * inv_rms * learner_gain).astype(jnp.bfloat16)
    frozen_normed = (xfloat * inv_rms * frozen_gain).astype(jnp.bfloat16)
    normed_all, frozen_all = in_one_piece((normed, frozen_normed), "tensor", 0, 1)
    gate_pre, up_pre, hidden, partial_learned = project_up(
        normed_all, learner_gate, learner_up, learner_down
    )
    frozen_partial = project_up(frozen_all, frozen_gate, frozen_up, frozen_down)[3]
    learned, frozen_out = sent_together(
        (partial_learned.astype(jnp.bfloat16), frozen_partial.astype(jnp.bfloat16)), "tensor", 0, 1
    )
    goal = targets.astype(jnp.float32)
    root = math.sqrt(tokens.shape[1])
    miss = learned - goal
    frozen_miss = frozen_out - goal
    learner_loss = 0.5 * jnp.sum(miss * miss, axis=-1) / root
    frozen_loss = 0.5 * jnp.sum(frozen_miss * frozen_miss, axis=-1) / root
    scores = learner_loss - frozen_loss
    weight = jax.nn.sigmoid(scores)
    out_grad = (weight[:, None] * miss / root).astype(jnp.bfloat16)
    grads_all = lax.all_gather(out_grad, "tensor", axis=0, tiled=True)
    hidden_grad = jnp.dot(grads_all, learner_down.T, preferred_element_type=jnp.float32)
    sigma = jax.nn.sigmoid(gate_pre)
    gate_grad = (hidden_grad * up_pre * sigma * (1.0 + gate_pre * (1.0 - sigma))).astype(
        jnp.bfloat16
    )
    up_grad = (hidden_grad * gate_pre * sigma).astype(jnp.bfloat16)
    partial_normed = jnp.dot(
        gate_grad, learner_gate.T, preferred_element_type=jnp.float32
    ) + jnp.dot(up_grad, learner_up.T, preferred_element_type=jnp.float32)
    normed_grad = sum_at_owner(partial_normed.astype(jnp.bfloat16), "tensor", 0)
    gain_term = jnp.sum(normed_grad * xfloat * inv_rms, axis=0)
    grad_gain = lax.psum(gain_term, ("dp", "tensor"))
    scaled = learner_gain * normed_grad
    cubed = inv_rms * inv_rms * inv_rms
    grad_tokens = (
        inv_rms * scaled - xfloat * cubed * jnp.mean(scaled * xfloat, axis=-1, keepdims=True)
    ).astype(jnp.bfloat16)
    gate_term = jnp.einsum("td,tf->df", normed_all, gate_grad, preferred_element_type=jnp.float32)
    up_term = jnp.einsum("td,tf->df", normed_all, up_grad, preferred_element_type=jnp.float32)
    down_term = jnp.einsum("td,tf->df", grads_all, hidden, preferred_element_type=jnp.float32)
    grad_gate, grad_up, down_shard = sent_together(
        (
            gate_term.astype(jnp.bfloat16),
            up_term.astype(jnp.bfloat16),
            down_term.astype(jnp.bfloat16),
        ),
        "dp",
        0,
        1,
    )
    grad_down = down_shard.T
    return (scores, grad_tokens, grad_gain, grad_gate, grad_up, grad_down)


def solution(mesh):
    placed = (
        P(("dp", "tensor"), None),
        P(("dp", "tensor"), None),
        P(),
        P(None, "tensor"),
        P(None, "tensor"),
        P("tensor", None),
        P(),
        P(None, "tensor"),
        P(None, "tensor"),
        P("tensor", None),
    )
    return jax.shard_map(
        local,
        mesh=mesh,
        in_specs=placed,
        out_specs=(
            P(("dp", "tensor")),
            P(("dp", "tensor"), None),
            P(),
            P("dp", "tensor"),
            P("dp", "tensor"),
            P("tensor", "dp"),
        ),
        check_vma=False,
    )
```

profile of v0, /device:TPU:1, one launch (start us, length us, event | category | flops | bytes accessed | tf_op | source)
XLA Modules:
  0.0 515.8 jit_solution(17087560783303499383)
XLA Ops:
  7.2 1.2 fusion.21
  8.5 1.1 fusion.17
  9.6 0.8 pad_maximum_fusion.2
  10.5 77.0 %all-gather.3.cloned.1.call-done = bf16[1024,4096]{1,0:T(8,128)(2,1)} async-done(((bf16[64,4096]{1,0:T(8,128)(2,1)}), bf16[1024,4096]{1,0:T(8,128)(2,1)}) %all-gather.3.cloned.1.call-update) | async-done | bytes 8388624 | tf_op jit(solution)/shard_map/all_gather | solution.py:10
  87.5 5.3 %fusion.8 = f32[1024,512]{1,0:T(8,128)S(1)} fusion(bf16[2048,512]{1,0:T(8,128)(2,1)} %param.13, bf16[1024,4096]{1,0:T(8,128)(2,1)} %all-gather.3.cloned.1.call-done), kind=kOutput, calls=%fused_computation.20 | convolution fusion | flops 2147483648 | bytes 8388608 | tf_op jit(solution)/shard_map/dot_general | solution.py:37
  93.4 3.8 multiply_convert_fusion.3
  97.2 4.3 convolution_convert_fusion.1
  101.5 3.7 fusion.2
  105.2 10.6 %convolution_convert_fusion = bf16[1024,2048]{1,0:T(8,128)(2,1)} fusion(bf16[512,2048]{1,0:T(8,128)(2,1)} %param.19, f32[1024,512]{1,0:T(8,128)} %fusion.2, bf16[2048,512]{1,0:T(8,128)(2,1)} %param.18, bf16[1024,4096]{1,0:T(8,128)(2,1)} %all-gather.3.cloned.1.call-done), kind=kOutput, calls=%fused_computation.7 | convolution fusion | flops 4300210176 | bytes 14680064 | tf_op jit(solution)/shard_map/dot_general | solution.py:40
  115.8 7.8 %pad_maximum_fusion = bf16[1024,4096]{1,0:T(8,128)(2,1)} fusion(bf16[1024,2048]{1,0:T(8,128)(2,1)} %convolution_convert_fusion, bf16[1024,2048]{1,0:T(8,128)(2,1)} %convolution_convert_fusion.1), kind=kLoop, calls=%fused_computation.2 | loop fusion | flops 16777216 | bytes 16777216 | tf_op jit(solution)/shard_map/concatenate | solution.py:31
  123.6 99.4 %all_to_all.15 = bf16[16,64,4096]{2,1,0:T(8,128)(2,1)S(1)} all-to-all(bf16[16,64,4096]{2,1,0:T(8,128)(2,1)} %bitcast.25), channel_id=1, replica_groups=mesh['dp'=8,'tensor'=16] {'tensor'}, dimensions={0} | all-to-all | bytes 16777216 | tf_op jit(solution)/shard_map/all_to_all | solution.py:25
  223.0 1.6 convert_reduce_fusion
  225.3 0.8 multiply_convert_fusion.4
  226.2 52.8 %all-gather.5.cloned.1.call-done = bf16[1024,2048]{1,0:T(8,128)(2,1)} async-done(((bf16[64,2048]{1,0:T(8,128)(2,1)}), bf16[1024,2048]{1,0:T(8,128)(2,1)}) %all-gather.5.cloned.1.call-update) | async-done | bytes 4194320 | tf_op jit(solution)/shard_map/all_gather | solution.py:77
  279.0 6.5 %multiply_convert_fusion = (bf16[1024,512]{1,0:T(8,128)(2,1)S(1)}, bf16[1024,512]{1,0:T(8,128)(2,1)S(1)}) fusion(f32[1024,512]{1,0:T(8,128)} %copy-done.13, f32[1024,512]{1,0:T(8,128)} %get-tuple-element.34, bf16[1024,2048]{1,0:T(8,128)(2,1)} %all-gather.5.cloned.1.call-done, bf16[512,2048]{1,0:T(8,128)(2,1)S(1)} %copy-done), kind=kOutput, calls=%fused_computation.22 | convolution fusion | flops 2154299392 | bytes 12582912 | tf_op jit(solution)/shard_map/dot_general | solution.py:78
  285.6 2.4 fusion.29
  288.0 4.3 add_convert_fusion
  292.3 4.7 all-to-all-start.1
  297.0 5.0 convolution_convert_fusion.2
  302.0 4.7 convolution_convert_fusion.3
  306.8 2.4 convolution_convert_fusion.4
  309.2 9.6 %pad_maximum_fusion.1 = bf16[2048,1536]{0,1:T(8,128)(2,1)S(1)} fusion(bf16[2048,512]{0,1:T(8,128)(2,1)S(1)} %convolution_convert_fusion.2, bf16[2048,512]{0,1:T(8,128)(2,1)S(1)} %convolution_convert_fusion.3, bf16[2048,512]{0,1:T(8,128)(2,1)S(1)} %convolution_convert_fusion.4), kind=kLoop, calls=%fused_computation.6 | loop fusion | flops 18874368 | bytes 12582912 | tf_op jit(solution)/shard_map/concatenate | solution.py:31
  318.8 3.1 copy.23
  321.9 25.9 %all-to-all-done.1 = bf16[16,64,2048]{2,1,0:T(8,128)(2,1)} async-done(((bf16[16,64,2048]{2,1,0:T(8,128)(2,1)}), bf16[16,64,2048]{2,1,0:T(8,128)(2,1)}, u32[]{:S(2)}, u32[]{:S(2)}) %all-to-all-start.1) | async-done | bytes 4194336 | tf_op jit(solution)/shard_map/all_to_all | solution.py:25
  347.8 5.0 all-to-all-start.2
  352.9 3.0 convert_reduce_fusion.2
  356.1 145.1 %psum.7 = f32[2048]{0:T(1024)} all-reduce(f32[2048]{0:T(1024)S(1)} %get-tuple-element.20), channel_id=1, replica_groups=mesh['dp'=8,'tensor'=16] {'dp','tensor'}, use_global_device_ids=true, to_apply=%region_7.8 | all-reduce | flops 2048 | bytes 16384 | tf_op jit(solution)/shard_map/psum | solution.py:89
  501.2 0.9 fusion.24
  502.2 3.9 convert_reduce_fusion.1
  506.1 0.9 slice_bitcast_fusion
  507.0 1.0 copy.20
  508.0 1.0 copy.19
  (43 shorter events, 1.6 us)
Async XLA Ops:
  7.2 90.0 %copy-start = (bf16[512,2048]{1,0:T(8,128)(2,1)S(1)}, bf16[512,2048]{1,0:T(8,128)(2,1)}, u32[]{:S(2)}) copy-start(bf16[512,2048]{1,0:T(8,128)(2,1)} %param.15) | copy-start | bytes 6291460
  7.2 80.3 %all-gather.3.cloned.1.call-start = ((), (), s32[]{:S(2)}) async-start(), calls=%async_computation.3 | async-start | bytes 8912896 | tf_op jit(solution)/shard_map/all_gather | solution.py:10
  10.5 268.5 %all-gather.5.cloned.1.call-start = ((), (), s32[]{:S(2)}) async-start(), calls=%async_computation.4 | async-start | bytes 4456448 | tf_op jit(solution)/shard_map/all_gather | solution.py:77
  87.5 5.3 %copy-start.5 = (bf16[1024,4096]{1,0:T(8,128)(2,1)S(1)}, bf16[1024,4096]{1,0:T(8,128)(2,1)}, u32[]{:S(2)}) copy-start(bf16[1024,4096]{1,0:T(8,128)(2,1)} %all-gather.3.cloned.1.call-done) | copy-start | bytes 25165828
  87.5 5.8 %copy-start.8 = (bf16[2048,512]{1,0:T(8,128)(2,1)S(1)}, bf16[2048,512]{1,0:T(8,128)(2,1)}, u32[]{:S(2)}) copy-start(bf16[2048,512]{1,0:T(8,128)(2,1)} %param.14) | copy-start | bytes 6291460
  93.4 3.8 copy-start.13
  97.2 4.3 copy-start.12
  97.2 4.3 copy-start.6
  223.0 1.6 copy-start.3
  279.0 6.6 %copy-start.7 = (bf16[2048,512]{1,0:T(8,128)(2,1)S(1)}, bf16[2048,512]{1,0:T(8,128)(2,1)}, u32[]{:S(2)}) copy-start(bf16[2048,512]{1,0:T(8,128)(2,1)} %param.13) | copy-start | bytes 6291460
  285.5 2.4 copy-start.10
  285.5 2.4 copy-start.9
  292.3 55.5 %all-to-all-start.1 = ((bf16[16,64,2048]{2,1,0:T(8,128)(2,1)}), bf16[16,64,2048]{2,1,0:T(8,128)(2,1)}, u32[]{:S(2)}, u32[]{:S(2)}) async-start(bf16[16,64,2048]{2,1,0:T(8,128)(2,1)} %bitcast.28), calls=%async_computation.1 | async-start | bytes 8388608 | tf_op jit(solution)/shard_map/all_to_all | solution.py:25
  296.9 9.8 %slice-start = ((s8[8388608]{0:T(1024)(128)(4,1)}), s8[4194304]{0:T(1024)(128)(4,1)S(1)}, s32[]{:S(2)}) async-start(s8[8388608]{0:T(1024)(128)(4,1)} %bitcast.29), calls=%async_computation.5 | async-start | bytes 8388608
  302.0 4.8 slice-start.1
  302.0 4.8 copy-start.11
  347.8 154.3 %all-to-all-start.2 = ((bf16[8,256,1536]{1,2,0:T(8,128)(2,1)}), bf16[8,256,1536]{1,2,0:T(8,128)(2,1)}, u32[]{:S(2)}, u32[]{:S(2)}) async-start(bf16[8,256,1536]{1,2,0:T(8,128)(2,1)} %bitcast.26), calls=%async_computation.2 | async-start | bytes 12582912 | tf_op jit(solution)/shard_map/all_to_all | solution.py:25
  352.8 3.1 copy-start.2
  352.8 3.1 copy-start.4
  502.2 6.8 %copy-start.1 = (bf16[512,2048]{1,0:T(8,128)(2,1)S(1)}, bf16[512,2048]{1,0:T(8,128)(2,1)}, u32[]{:S(2)}) copy-start(bf16[512,2048]{1,0:T(8,128)(2,1)} %param.15) | copy-start | bytes 6291460
Sparse Core Ops, SparseCore 0:
  11.0 76.4 all-gather.2
  226.3 52.6 all-gather.4
where the time goes:
time: 516 us
  blocking collectives  245 us (47%)
  waiting for transfers between devices  156 us (30%)
  matrix products  53.1 us (10%)
  other arithmetic  31.9 us (6%)
  between operations  14.3 us (3%)
  starting transfers between devices  9.77 us (2%)
  local copies, waits for them, and re-layouts  6.52 us (1%)
    psum x1, blocking collectives, local(): grad_gain = lax.psum(gain_term, ('dp', 'tensor'))  145 us
    all_to_all x1, blocking collectives, sum_at_owner(): lax.all_to_all(blocks, axis, split_axis=0, concat_axis=0, tiled=True)  99.4 us
    all_gather x1, waiting for transfers between devices, in_one_piece(): lax.all_gather(both, axis, axis=dim, tiled=True)  77 us
    all_gather x1, waiting for transfers between devices, local(): grads_all = lax.all_gather(out_grad, 'tensor', axis=0, tiled=True)  52.8 us
    all_to_all x2, waiting for transfers between devices, sum_at_owner(): lax.all_to_all(blocks, axis, split_axis=0, concat_axis=0, tiled=True)  25.9 us
    concatenate x2, other arithmetic, sent_together(): both = jnp.concatenate(arrays, axis=along)  17.4 us
    dot_general x2, matrix products, project_up(): partial_out = jnp.dot(hidden, w_down, preferred_element_type=jnp.float32)  14.9 us
  transfers between devices with their start and end apart: 4, of which 3 were waited for; matrix products, arithmetic and copies ran while one was open for 6% of the time, Pallas kernels for 0%

commit v1 on v0

--- a/solution.py
+++ b/solution.py
@@ -86,7 +86,7 @@
     ) + jnp.dot(up_grad, learner_up.T, preferred_element_type=jnp.float32)
     normed_grad = sum_at_owner(partial_normed.astype(jnp.bfloat16), "tensor", 0)
     gain_term = jnp.sum(normed_grad * xfloat * inv_rms, axis=0)
-    grad_gain = lax.psum(gain_term, ("dp", "tensor"))
+    grad_gain = lax.psum(lax.psum(gain_term, "tensor"), "dp")
     scaled = learner_gain * normed_grad
     cubed = inv_rms * inv_rms * inv_rms
     grad_tokens = (

time: 516 us -> 484 us (0.938); the launches traced: 516 us -> 476 us
  blocking collectives: 245 us -> 205 us
    psum x1 -> x2, blocking collectives: 145 us -> 105 us  [local(): grad_gain = lax.psum(lax.psum(gain_term, 'tensor'), 'dp')]
where the time goes in v1:
time: 484 us; the launch traced here: 476 us
  blocking collectives  205 us (42%)
  waiting for transfers between devices  156 us (32%)
  matrix products  53.1 us (11%)
  other arithmetic  31.9 us (7%)
  between operations  14.3 us (3%)
  starting transfers between devices  9.52 us (2%)
  local copies, waits for them, and re-layouts  6.52 us (1%)
    psum x2, blocking collectives, local(): grad_gain = lax.psum(lax.psum(gain_term, 'tensor'), 'dp')  105 us
    all_to_all x1, blocking collectives, sum_at_owner(): lax.all_to_all(blocks, axis, split_axis=0, concat_axis=0, tiled=True)  99.4 us
    all_gather x1, waiting for transfers between devices, in_one_piece(): lax.all_gather(both, axis, axis=dim, tiled=True)  77 us
    all_gather x1, waiting for transfers between devices, local(): grads_all = lax.all_gather(out_grad, 'tensor', axis=0, tiled=True)  52.8 us
    all_to_all x2, waiting for transfers between devices, sum_at_owner(): lax.all_to_all(blocks, axis, split_axis=0, concat_axis=0, tiled=True)  25.9 us
    concatenate x2, other arithmetic, sent_together(): both = jnp.concatenate(arrays, axis=along)  17.4 us
    dot_general x2, matrix products, project_up(): partial_out = jnp.dot(hidden, w_down, preferred_element_type=jnp.float32)  14.9 us
  transfers between devices with their start and end apart: 4, of which 3 were waited for; matrix products, arithmetic and copies ran while one was open for 6% of the time, Pallas kernels for 0%

profile of v1, /device:TPU:1, one launch (start us, length us, event | category | flops | bytes accessed | tf_op | source)
XLA Modules:
  0.0 475.6 jit_solution(14510077146409072441)
XLA Ops:
  7.2 1.2 fusion.21
  8.5 1.1 fusion.17
  9.6 0.8 pad_maximum_fusion.2
  10.5 77.0 %all-gather.3.cloned.1.call-done = bf16[1024,4096]{1,0:T(8,128)(2,1)} async-done(((bf16[64,4096]{1,0:T(8,128)(2,1)}), bf16[1024,4096]{1,0:T(8,128)(2,1)}) %all-gather.3.cloned.1.call-update) | async-done | bytes 8388624 | tf_op jit(solution)/shard_map/all_gather | solution.py:10
  87.5 5.3 %fusion.8 = f32[1024,512]{1,0:T(8,128)S(1)} fusion(bf16[2048,512]{1,0:T(8,128)(2,1)} %param.13, bf16[1024,4096]{1,0:T(8,128)(2,1)} %all-gather.3.cloned.1.call-done), kind=kOutput, calls=%fused_computation.20 | convolution fusion | flops 2147483648 | bytes 8388608 | tf_op jit(solution)/shard_map/dot_general | solution.py:37
  93.4 3.8 multiply_convert_fusion.3
  97.2 4.3 convolution_convert_fusion.1
  101.5 3.7 fusion.2
  105.2 10.6 %convolution_convert_fusion = bf16[1024,2048]{1,0:T(8,128)(2,1)} fusion(bf16[512,2048]{1,0:T(8,128)(2,1)} %param.19, f32[1024,512]{1,0:T(8,128)} %fusion.2, bf16[2048,512]{1,0:T(8,128)(2,1)} %param.18, bf16[1024,4096]{1,0:T(8,128)(2,1)} %all-gather.3.cloned.1.call-done), kind=kOutput, calls=%fused_computation.7 | convolution fusion | flops 4300210176 | bytes 14680064 | tf_op jit(solution)/shard_map/dot_general | solution.py:40
  115.8 7.8 %pad_maximum_fusion = bf16[1024,4096]{1,0:T(8,128)(2,1)} fusion(bf16[1024,2048]{1,0:T(8,128)(2,1)} %convolution_convert_fusion, bf16[1024,2048]{1,0:T(8,128)(2,1)} %convolution_convert_fusion.1), kind=kLoop, calls=%fused_computation.2 | loop fusion | flops 16777216 | bytes 16777216 | tf_op jit(solution)/shard_map/concatenate | solution.py:31
  123.6 99.4 %all_to_all.15 = bf16[16,64,4096]{2,1,0:T(8,128)(2,1)S(1)} all-to-all(bf16[16,64,4096]{2,1,0:T(8,128)(2,1)} %bitcast.25), channel_id=1, replica_groups=mesh['dp'=8,'tensor'=16] {'tensor'}, dimensions={0} | all-to-all | bytes 16777216 | tf_op jit(solution)/shard_map/all_to_all | solution.py:25
  223.0 1.6 convert_reduce_fusion
  226.2 52.8 %all-gather.5.cloned.1.call-done = bf16[1024,2048]{1,0:T(8,128)(2,1)} async-done(((bf16[64,2048]{1,0:T(8,128)(2,1)}), bf16[1024,2048]{1,0:T(8,128)(2,1)}) %all-gather.5.cloned.1.call-update) | async-done | bytes 4194320 | tf_op jit(solution)/shard_map/all_gather | solution.py:77
  279.0 6.5 %multiply_convert_fusion = (bf16[1024,512]{1,0:T(8,128)(2,1)S(1)}, bf16[1024,512]{1,0:T(8,128)(2,1)S(1)}) fusion(f32[1024,512]{1,0:T(8,128)} %copy-done.13, f32[1024,512]{1,0:T(8,128)} %get-tuple-element.34, bf16[1024,2048]{1,0:T(8,128)(2,1)} %all-gather.5.cloned.1.call-done, bf16[512,2048]{1,0:T(8,128)(2,1)S(1)} %copy-done), kind=kOutput, calls=%fused_computation.22 | convolution fusion | flops 2154299392 | bytes 12582912 | tf_op jit(solution)/shard_map/dot_general | solution.py:78
  285.5 2.4 fusion.29
  287.9 4.3 add_convert_fusion
  292.2 4.7 all-to-all-start.1
  297.0 5.0 %convolution_convert_fusion.2 = bf16[2048,512]{0,1:T(8,128)(2,1)S(1)} fusion(bf16[1024,2048]{1,0:T(8,128)(2,1)} %all-gather.5.cloned.1.call-done, bf16[1024,512]{1,0:T(8,128)(2,1)} %copy-done.12), kind=kOutput, calls=%fused_computation.13 | convolution fusion | flops 2148532224 | bytes 7340032 | tf_op jit(solution)/shard_map/td,tf->df/dot_general | solution.py:97
  302.0 4.7 convolution_convert_fusion.3
  306.8 2.4 convolution_convert_fusion.4
  309.2 9.6 %pad_maximum_fusion.1 = bf16[2048,1536]{0,1:T(8,128)(2,1)S(1)} fusion(bf16[2048,512]{0,1:T(8,128)(2,1)S(1)} %convolution_convert_fusion.2, bf16[2048,512]{0,1:T(8,128)(2,1)S(1)} %convolution_convert_fusion.3, bf16[2048,512]{0,1:T(8,128)(2,1)S(1)} %convolution_convert_fusion.4), kind=kLoop, calls=%fused_computation.6 | loop fusion | flops 18874368 | bytes 12582912 | tf_op jit(solution)/shard_map/concatenate | solution.py:31
  318.8 3.1 copy.23
  321.9 25.9 %all-to-all-done.1 = bf16[16,64,2048]{2,1,0:T(8,128)(2,1)} async-done(((bf16[16,64,2048]{2,1,0:T(8,128)(2,1)}), bf16[16,64,2048]{2,1,0:T(8,128)(2,1)}, u32[]{:S(2)}, u32[]{:S(2)}) %all-to-all-start.1) | async-done | bytes 4194336 | tf_op jit(solution)/shard_map/all_to_all | solution.py:25
  347.8 4.8 all-to-all-start.2
  352.6 3.0 convert_reduce_fusion.2
  355.8 82.0 %psum.14 = f32[2048]{0:T(1024)S(1)} all-reduce(f32[2048]{0:T(1024)S(1)} %get-tuple-element.20), channel_id=1, replica_groups=mesh['dp'=8,'tensor'=16] {'tensor'}, use_global_device_ids=true, to_apply=%region_7.8 | all-reduce | flops 2048 | bytes 16384 | tf_op jit(solution)/shard_map/psum | solution.py:89
  437.8 23.2 %psum.15 = f32[2048]{0:T(1024)} all-reduce(f32[2048]{0:T(1024)S(1)} %psum.14), channel_id=1, replica_groups=mesh['dp'=8,'tensor'=16] {'dp'}, use_global_device_ids=true, to_apply=%region_8.9 | all-reduce | flops 2048 | bytes 16384 | tf_op jit(solution)/shard_map/psum | solution.py:89
  461.0 0.9 fusion.24
  461.9 3.9 convert_reduce_fusion.1
  465.9 0.9 slice_bitcast_fusion
  466.8 1.0 copy.20
  467.8 1.0 copy.19
  (44 shorter events, 2.4 us)
Async XLA Ops:
  7.2 90.0 %copy-start = (bf16[512,2048]{1,0:T(8,128)(2,1)S(1)}, bf16[512,2048]{1,0:T(8,128)(2,1)}, u32[]{:S(2)}) copy-start(bf16[512,2048]{1,0:T(8,128)(2,1)} %param.15) | copy-start | bytes 6291460
  7.2 80.3 %all-gather.3.cloned.1.call-start = ((), (), s32[]{:S(2)}) async-start(), calls=%async_computation.3 | async-start | bytes 8912896 | tf_op jit(solution)/shard_map/all_gather | solution.py:10
  10.5 268.5 %all-gather.5.cloned.1.call-start = ((), (), s32[]{:S(2)}) async-start(), calls=%async_computation.4 | async-start | bytes 4456448 | tf_op jit(solution)/shard_map/all_gather | solution.py:77
  87.5 5.3 %copy-start.5 = (bf16[1024,4096]{1,0:T(8,128)(2,1)S(1)}, bf16[1024,4096]{1,0:T(8,128)(2,1)}, u32[]{:S(2)}) copy-start(bf16[1024,4096]{1,0:T(8,128)(2,1)} %all-gather.3.cloned.1.call-done) | copy-start | bytes 25165828
  87.5 5.8 %copy-start.8 = (bf16[2048,512]{1,0:T(8,128)(2,1)S(1)}, bf16[2048,512]{1,0:T(8,128)(2,1)}, u32[]{:S(2)}) copy-start(bf16[2048,512]{1,0:T(8,128)(2,1)} %param.14) | copy-start | bytes 6291460
  93.4 3.8 copy-start.13
  97.2 4.3 copy-start.12
  97.2 4.3 copy-start.6
  223.0 1.6 copy-start.3
  279.0 6.6 %copy-start.7 = (bf16[2048,512]{1,0:T(8,128)(2,1)S(1)}, bf16[2048,512]{1,0:T(8,128)(2,1)}, u32[]{:S(2)}) copy-start(bf16[2048,512]{1,0:T(8,128)(2,1)} %param.13) | copy-start | bytes 6291460
  285.5 2.4 copy-start.10
  285.5 2.4 copy-start.9
  292.2 55.6 %all-to-all-start.1 = ((bf16[16,64,2048]{2,1,0:T(8,128)(2,1)}), bf16[16,64,2048]{2,1,0:T(8,128)(2,1)}, u32[]{:S(2)}, u32[]{:S(2)}) async-start(bf16[16,64,2048]{2,1,0:T(8,128)(2,1)} %bitcast.28), calls=%async_computation.1 | async-start | bytes 8388608 | tf_op jit(solution)/shard_map/all_to_all | solution.py:25
  296.9 9.8 %slice-start = ((s8[8388608]{0:T(1024)(128)(4,1)}), s8[4194304]{0:T(1024)(128)(4,1)S(1)}, s32[]{:S(2)}) async-start(s8[8388608]{0:T(1024)(128)(4,1)} %bitcast.29), calls=%async_computation.5 | async-start | bytes 8388608
  302.0 4.8 %slice-start.1 = ((s8[8388608]{0:T(1024)(128)(4,1)}), s8[4194304]{0:T(1024)(128)(4,1)S(1)}, s32[]{:S(2)}) async-start(s8[8388608]{0:T(1024)(128)(4,1)} %bitcast.29), calls=%async_computation.6 | async-start | bytes 8388608
  302.0 4.8 %copy-start.11 = (bf16[1024,512]{1,0:T(8,128)(2,1)S(1)}, bf16[1024,512]{1,0:T(8,128)(2,1)}, u32[]{:S(2)}) copy-start(bf16[1024,512]{1,0:T(8,128)(2,1)} %copy-done.10) | copy-start | bytes 3145732
  347.8 114.1 %all-to-all-start.2 = ((bf16[8,256,1536]{1,2,0:T(8,128)(2,1)}), bf16[8,256,1536]{1,2,0:T(8,128)(2,1)}, u32[]{:S(2)}, u32[]{:S(2)}) async-start(bf16[8,256,1536]{1,2,0:T(8,128)(2,1)} %bitcast.26), calls=%async_computation.2 | async-start | bytes 12582912 | tf_op jit(solution)/shard_map/all_to_all | solution.py:25
  352.6 3.1 copy-start.2
  352.6 3.1 copy-start.4
  461.9 6.8 %copy-start.1 = (bf16[512,2048]{1,0:T(8,128)(2,1)S(1)}, bf16[512,2048]{1,0:T(8,128)(2,1)}, u32[]{:S(2)}) copy-start(bf16[512,2048]{1,0:T(8,128)(2,1)} %param.15) | copy-start | bytes 6291460
Sparse Core Ops, SparseCore 0:
  11.0 76.4 all-gather.2
  226.3 52.6 all-gather.4
